TPU v7x, 256 devices: a whole 4x4x8 slice. The times are simulated.
256 devices in a mesh: lat: 8 (over x, core), lon: 32 (over y, z).
Axes of the slice: x: 4, y: 4, z: 8, core: 2. Of those that a mesh axis runs over, the one named last changes fastest.
Arguments:
- prediction_fields: float32 [4, 69, 1440, 1024], P(None, None, 'lon', 'lat'), may hold values from -16 to 16
- verifying_state: float32 [69, 1440, 1024], P(None, 'lon', 'lat'), may hold values from -16 to 16
- normal_state: float32 [69, 1440, 1024], P(None, 'lon', 'lat'), may hold values from -16 to 16
- evaluated_point_flag: int32 [1440, 1024], P('lon', 'lat'), may hold values 0 or 1
- parallels_each_strip: int32 [8], replicated, may hold values from 1 to 128, 721 in all
Outputs:
- parallel_quadratic_error: float32 [4, 69, 1024], P(None, None, 'lat')
- parallel_systematic_error: float32 [4, 69, 1024], P(None, None, 'lat')
- parallel_pattern_skill: float32 [4, 69, 1024], P(None, None, 'lat')
- rmse: float32 [4, 69], replicated
- systematic_error: float32 [4, 69], replicated
- pattern_skill: float32 [4, 69], replicated
Inputs may be any that keep to these rules, and one draw needn't show every extreme that they name: `parallels_each_strip`: they sum to 721, and some band holds exactly 128 rows.
All inputs are finite; a program needn't handle non-finite values.
Results may differ from a plain program's by a relative error of at most 0.00002.
Values sent between devices are 32-bit elements.
A program may use at most 64 MiB of HBM per device.

v0:
```python
import functools

import jax
import jax.numpy as jnp
from jax import lax
from jax.sharding import Mesh
from jax.sharding import PartitionSpec as P

MEAN_ROWS = 90
LAT = ("lat_0", "lat_1")
LON = ("lon_0", "lon_1")
LAT_LON = ("lat_0", "lat_1", "lon_0", "lon_1")


minimum_divisor = 0.1


def by_axis(shard, axes):
    return functools.reduce(lax.psum, axes, shard)


def split_up(shard, dim, devices):
    dims = shard.shape
    tiles = shard.reshape(*dims[:dim], devices, dims[dim] // devices, *dims[dim + 1 :])
    return jnp.moveaxis(tiles, dim, 0)


def sent_and_summed(shard, axis, dim):
    devices = lax.axis_size(axis)
    tiles = lax.all_to_all(split_up(shard, dim, devices), axis, 0, 0, tiled=True)
    return jnp.sum(tiles, axis=0)


def gather_turned(arrays, axis, dims):
    turned = [jnp.moveaxis(a, dim, 0) for a, dim in zip(arrays, dims)]
    both = jnp.concatenate([t.reshape(len(t), -1) for t in turned], axis=1)
    filled, at, done = (lax.all_gather(both, axis, axis=0, tiled=True), 0, [])
    for t, dim in zip(turned, dims):
        slab = filled[:, at : at + t[0].size].reshape(-1, *t.shape[1:])
        done.append(jnp.moveaxis(slab, 0, dim))
        at += t[0].size
    return tuple(done)


def stacked_metrics(totals, horizon_tally, quantity_tally, grid_point_tally):
    block_rows = horizon_tally * quantity_tally
    width = totals.shape[1]
    error_power_two = (
        totals[:block_rows].reshape(horizon_tally, quantity_tally, width) / grid_point_tally
    )
    prediction_error = (
        totals[block_rows : 2 * block_rows].reshape(horizon_tally, quantity_tally, width)
        / grid_point_tally
    )
    paired_anomaly_term = (
        totals[2 * block_rows : 3 * block_rows].reshape(horizon_tally, quantity_tally, width)
        / grid_point_tally
    )
    predicted_spread_sum = (
        totals[3 * block_rows : 4 * block_rows].reshape(horizon_tally, quantity_tally, width)
        / grid_point_tally
    )
    observed_dispersion = (
        totals[4 * block_rows :].reshape(1, quantity_tally, width) / grid_point_tally
    )
    divisor_term = jnp.sqrt(
        jnp.maximum(predicted_spread_sum, minimum_divisor)
        * jnp.maximum(observed_dispersion, minimum_divisor)
    )
    return (error_power_two, prediction_error, paired_anomaly_term / divisor_term)


def local(
    prediction_fields, verifying_state, normal_state, evaluated_point_flag, parallels_each_strip
):
    horizon_tally, quantity_tally, zonal_circle_size, parallel_index = prediction_fields.shape
    lat_bands = lax.axis_size(LAT)
    lon_spokes = lax.axis_size(LON)
    lat_total = MEAN_ROWS * lat_bands + 1
    lon_total = zonal_circle_size * lon_spokes
    band_index = lax.axis_index(LAT)
    band_ids = jnp.arange(lat_bands, dtype=jnp.int32)
    first_row = jnp.sum(jnp.where(band_ids < band_index, parallels_each_strip, 0))
    band_filled = jnp.sum(jnp.where(band_ids == band_index, parallels_each_strip, 0))
    slot_ids = jnp.arange(parallel_index, dtype=jnp.int32)
    inside_band = slot_ids < band_filled
    angles = jnp.pi * jnp.arange(lat_total, dtype=jnp.float32) / (lat_total - 1)
    normalizer = jnp.sum(jnp.sin(angles))
    row_angle = jnp.pi * (first_row + slot_ids).astype(jnp.float32) / (lat_total - 1)
    area_factors = jnp.where(inside_band, jnp.sin(row_angle) * lat_total / normalizer, 0.0)
    retain_filter = (
        evaluated_point_flag.astype(jnp.float32) * inside_band.astype(jnp.float32)[None, :]
    )
    observed_anomaly = verifying_state - normal_state
    predicted_anomaly = prediction_fields - normal_state[None]
    mistake_field = predicted_anomaly - observed_anomaly[None]
    retained_entries = retain_filter[None, None]
    block_rows = horizon_tally * quantity_tally
    partial_value = jnp.concatenate(
        [
            jnp.sum(retained_entries * mistake_field * mistake_field, axis=2).reshape(
                block_rows, parallel_index
            ),
            jnp.sum(retained_entries * mistake_field, axis=2).reshape(block_rows, parallel_index),
            jnp.sum(retained_entries * predicted_anomaly * observed_anomaly[None], axis=2).reshape(
                block_rows, parallel_index
            ),
            jnp.sum(retained_entries * predicted_anomaly * predicted_anomaly, axis=2).reshape(
                block_rows, parallel_index
            ),
            jnp.sum(retain_filter[None] * observed_anomaly * observed_anomaly, axis=1),
        ],
        axis=0,
    )
    grand = by_axis(jnp.sum(partial_value * area_factors, axis=1), LAT_LON)
    shares = sent_and_summed(partial_value, LON, 1)
    scores = stacked_metrics(shares, horizon_tally, quantity_tally, float(lon_total))
    error_power_two, prediction_error, covariance_sum = gather_turned(
        (scores[0], scores[1], scores[2]), LON, (2, 2, 2)
    )
    total_square, total_offset, total_agree = stacked_metrics(
        grand[:, None], horizon_tally, quantity_tally, float(lat_total * lon_total)
    )
    rmse = jnp.sqrt(jnp.maximum(total_square[:, :, 0], minimum_divisor))
    return (
        error_power_two,
        prediction_error,
        covariance_sum,
        rmse,
        total_offset[:, :, 0],
        total_agree[:, :, 0],
    )


def solution(mesh):
    split = Mesh(mesh.devices.reshape(4, 2, 4, 8), ("lat_0", "lat_1", "lon_0", "lon_1"))
    placed = (P(None, None, LON, LAT), P(None, LON, LAT), P(None, LON, LAT), P(LON, LAT), P())
    return jax.shard_map(
        local,
        mesh=split,
        in_specs=placed,
        out_specs=(P(None, None, LAT), P(None, None, LAT), P(None, None, LAT), P(), P(), P()),
        check_vma=False,
    )
```

profile of v0, /device:TPU:2, one launch (start us, length us, event | category | flops | bytes accessed | tf_op | source)
XLA Modules:
  0.0 129.2 jit_solution(12620161045907325382)
XLA Ops:
  0.6 1.3 %fusion.10 = (s32[]{:T(128)}, s32[]{:T(128)}) fusion(s32[8]{0:T(128)} %param.9, s32[]{:T(128)S(6)} %add.21), kind=kLoop, calls=%fused_computation.34 | loop fusion | flops 46 | bytes 44 | tf_op jit(solution)/shard_map/reduce_sum | solution.py:83
  1.9 0.6 compare_convert_fusion
  2.6 1.9 %copy.26 = f32[69,45,128]{2,1,0:T(8,128)S(1)} copy(f32[69,45,128]{2,0,1:T(8,128)} %param.7) | data formatting | bytes 3179520 | tf_op args[2]
  4.6 0.5 copy-done.2
  5.0 0.3 fusion.3
  5.4 0.3 copy.27
  5.7 2.2 %copy-done.1 = f32[4,69,45,128]{3,0,2,1:T(4,128)S(1)} copy-done((f32[4,69,45,128]{3,0,2,1:T(4,128)S(1)}, f32[4,69,45,128]{3,0,2,1:T(4,128)}, u32[]{:S(2)}) %copy-start.1) | copy-done | bytes 6359064
  7.8 10.2 %fusion.1 = (f32[4,69,128]{2,0,1:T(4,128)S(1)}, f32[4,69,128]{2,0,1:T(4,128)S(1)}, f32[4,69,128]{2,0,1:T(4,128)S(1)}, f32[4,69,128]{2,0,1:T(4,128)S(1)}) fusion(f32[4,69,45,128]{3,0,2,1:T(4,128)S(1)} %copy-done.1, f32[69,45,128]{2,1,0:T(8,128)S(1)} %copy.27, f32[69,45,128]{2,1,0:T(8,128)S(1)} %copy.26, f32[45,128]{1,0:T(8,128)S(1)} %convert_multiply_fusion), kind=kLoop, calls=%fused_computation.5 | loop fusion | flops 17346048 | bytes 10126848 | tf_op jit(solution)/shard_map/reduce_sum | solution.py:105
  18.0 0.2 copy.28
  18.2 0.2 concatenate.19
  18.4 0.2 copy.29
  18.6 0.2 concatenate.20
  18.8 0.2 copy.30
  19.0 0.2 concatenate.21
  19.2 0.2 copy.31
  19.4 0.2 concatenate.22
  19.6 0.1 copy.32
  19.7 1.5 %concatenate.24 = f32[1173,32,4]{0,2,1:T(4,128)} concatenate(f32[276,32,4]{0,2,1:T(4,128)S(1)} %concatenate.19, f32[276,32,4]{0,2,1:T(4,128)S(1)} %concatenate.20, f32[276,32,4]{0,2,1:T(4,128)S(1)} %concatenate.21, f32[276,32,4]{0,2,1:T(4,128)S(1)} %concatenate.22, f32[69,32,4]{0,2,1:T(4,128)S(1)} %bitcast.36), dimensions={0} | concatenate | bytes 1201152 | tf_op jit(solution)/shard_map/concatenate | solution.py:99
  21.2 11.5 %all-to-all-start = ((f32[32,1173,4]{1,2,0:T(4,128)}), f32[32,1173,4]{1,2,0:T(4,128)S(1)}, u32[]{:S(2)}, u32[]{:S(2)}) async-start(f32[32,1173,4]{1,2,0:T(4,128)} %bitcast.1), calls=%async_computation | async-start | bytes 1310720 | tf_op jit(solution)/shard_map/all_to_all | solution.py:30
  32.8 0.7 concatenate.26
  33.5 0.6 sine_reduce_fusion
  34.1 2.0 %compare_select_fusion.2 = f32[128]{0:T(128)S(1)} fusion(f32[]{:T(128)} %sine_reduce_fusion, s32[]{:T(128)} %get-tuple-element.22, s32[]{:T(128)} %get-tuple-element.23), kind=kLoop, calls=%fused_computation.31 | loop fusion | flops 896 | bytes 524 | tf_op jit(solution)/shard_map/jit(_where)/select_n | solution.py:90
  36.1 0.2 multiply_reduce_fusion.1
  36.4 8.7 %psum.28 = f32[1173]{0:T(1024)S(1)} all-reduce(f32[1173]{0:T(1024)S(1)} %multiply_reduce_fusion.1), channel_id=1, replica_groups=mesh['lat_0'=4,'lat_1'=2,'lon_0'=4,'lon_1'=8] {'lat_0'}, use_global_device_ids=true, to_apply=%region_10.11 | all-reduce | flops 1173 | bytes 9384 | tf_op jit(solution)/shard_map/psum | solution.py:19
  45.1 2.5 %psum.29 = f32[1173]{0:T(1024)S(1)} all-reduce(f32[1173]{0:T(1024)S(1)} %psum.28), channel_id=1, replica_groups=mesh['lat_0'=4,'lat_1'=2,'lon_0'=4,'lon_1'=8] {'lat_1'}, use_global_device_ids=true, to_apply=%region_11.12 | all-reduce | flops 1173 | bytes 9384 | tf_op jit(solution)/shard_map/psum | solution.py:19
  47.6 10.9 %psum.30 = f32[1173]{0:T(1024)S(1)} all-reduce(f32[1173]{0:T(1024)S(1)} %psum.29), channel_id=1, replica_groups=mesh['lat_0'=4,'lat_1'=2,'lon_0'=4,'lon_1'=8] {'lon_0'}, use_global_device_ids=true, to_apply=%region_12.13 | all-reduce | flops 1173 | bytes 9384 | tf_op jit(solution)/shard_map/psum | solution.py:19
  58.5 17.1 %psum.31 = f32[1173]{0:T(1024)S(1)} all-reduce(f32[1173]{0:T(1024)S(1)} %psum.30), channel_id=1, replica_groups=mesh['lat_0'=4,'lat_1'=2,'lon_0'=4,'lon_1'=8] {'lon_1'}, use_global_device_ids=true, to_apply=%region_13.14 | all-reduce | flops 1173 | bytes 9384 | tf_op jit(solution)/shard_map/psum | solution.py:19
  75.7 0.1 div.94
  75.9 0.7 div.92
  76.5 0.7 sqrt.14
  77.3 0.6 rsqrt_multiply_fusion
  77.9 0.1 reduce_sum.96
  78.1 0.1 div.79
  78.2 0.1 max.42
  78.3 0.1 reshape.183
  78.5 0.1 reshape.181
  78.6 0.1 div.77
  78.7 0.1 reshape.182
  78.7 0.1 maximum_bitcast_fusion
  78.8 47.5 %all-gather = f32[32,4,828]{2,1,0:T(4,128)S(1)} all-gather(f32[1,4,828]{2,1,0:T(4,128)S(1)} %maximum_bitcast_fusion), channel_id=1, replica_groups=mesh['lat_0'=4,'lat_1'=2,'lon_0'=4,'lon_1'=8] {'lon_0','lon_1'}, dimensions={0}, use_global_device_ids=true | all-gather | bytes 437184 | tf_op jit(solution)/shard_map/all_gather | solution.py:37
  126.4 0.2 reshape.192
  126.5 0.2 fusion.12
  126.7 0.1 copy.33
  126.8 0.7 copy.40
  127.5 0.1 copy.34
  127.7 0.7 copy.41
  128.4 0.1 copy.35
  128.5 0.7 copy.42
  (26 shorter events, 0.6 us)
Async XLA Ops:
  0.6 3.9 %copy-start.3 = (s32[45,128]{1,0:T(8,128)S(1)}, s32[45,128]{1,0:T(8,128)}, u32[]{:S(2)}) copy-start(s32[45,128]{1,0:T(8,128)} %param.8) | copy-start | bytes 69124
  2.6 2.0 %copy-start = (f32[69,45,128]{2,0,1:T(8,128)S(1)}, f32[69,45,128]{2,0,1:T(8,128)}, u32[]{:S(2)}) copy-start(f32[69,45,128]{2,0,1:T(8,128)} %param.7) | copy-start | bytes 4769284
  2.6 2.4 %copy-start.2 = (f32[69,45,128]{2,0,1:T(8,128)S(1)}, f32[69,45,128]{2,0,1:T(8,128)}, u32[]{:S(2)}) copy-start(f32[69,45,128]{2,0,1:T(8,128)} %param.6) | copy-start | bytes 4769284
  5.0 2.8 %copy-start.1 = (f32[4,69,45,128]{3,0,2,1:T(4,128)S(1)}, f32[4,69,45,128]{3,0,2,1:T(4,128)}, u32[]{:S(2)}) copy-start(f32[4,69,45,128]{3,0,2,1:T(4,128)} %param.5) | copy-start | bytes 19077124
  21.2 56.7 %all-to-all-start = ((f32[32,1173,4]{1,2,0:T(4,128)}), f32[32,1173,4]{1,2,0:T(4,128)S(1)}, u32[]{:S(2)}, u32[]{:S(2)}) async-start(f32[32,1173,4]{1,2,0:T(4,128)} %bitcast.1), calls=%async_computation | async-start | bytes 1310720 | tf_op jit(solution)/shard_map/all_to_all | solution.py:30
where the time goes:
time: 131 us; the launch traced here: 129 us
  blocking collectives  86.8 us (66%)
  other arithmetic  16.4 us (13%)
  local copies, waits for them, and re-layouts  13.6 us (10%)
  starting transfers between devices  11.5 us (9%)
    all_gather x1, blocking collectives, gather_turned(): filled, at, done = (lax.all_gather(both, axis, axis=0, tiled=True), 0, [])  47.5 us
    psum x4, blocking collectives, by_axis(): return functools.reduce(lax.psum, axes, shard)  39.2 us
    all_to_all x1, starting transfers between devices, sent_and_summed(): lax.all_to_all(split_up(shard, dim, devices), axis, 0, 0, tiled=True)  11.5 us
    reduce_sum x1, other arithmetic, local(): jnp.sum(retained_entries * predicted_anomaly * observed_anomaly[None], ax...  10.2 us
    unnamed x13, local copies, waits for them, and re-layouts  6.8 us
    concatenate x6, local copies, waits for them, and re-layouts, local(): jnp.concatenate([jnp.sum(retained_entries * mistake_field * mistake_field...  3.03 us
  transfers between devices with their start and end apart: 1, of which 0 were waited for; matrix products, arithmetic and copies ran while one was open for 5% of the time, Pallas kernels for 0%

commit v1 on v0

v1 whole, which is shorter than its diff:
```python
import functools
import math

import jax
import jax.numpy as jnp
from jax import lax
from jax.experimental import pallas as pl
from jax.experimental.pallas import tpu as pltpu
from jax.sharding import PartitionSpec as P

MESH = pl.DeviceIdType.MESH
Y, Z = 4, 8
LEADS, VARS = 4, 69
GV = 18
PAIRS = 9
ROWS = 4 * PAIRS + 3
SCORES = 3 * PAIRS
OFFS = (4, 3, 5, 2, 6, 1, 7, 0)
NLAT, NLON = 721, 1440
FLOOR = 0.1
SIN_SUM = sum(math.sin(math.pi * g / (NLAT - 1)) for g in range(NLAT))


def kernel(p, t, n, flag, bands, o0, o1, o2, g0, g1, g2,
           pbuf, tbuf, nbuf, kbuf, wbuf, part, rel, in_m, in_p, zin, sbuf, gath, lin, hall,
           isem, rel_s, rel_r, dir_s, fwd_s, m_r, p_r, z_s, z_r, a_s, a_r, ym_s, yp_s, ym_r, yp_r,
           opp_s, opp_r, l_s, l_r, h_s, h_r):
    lat, j = lax.axis_index("lat"), lax.axis_index("lon")
    nlat = 8
    y, z = j // Z, lax.rem(j, Z)
    up, down = lax.rem(y + 1, Y), lax.rem(y + Y - 1, Y)
    f32 = jnp.float32

    def at(yy, zz):
        return yy * Z + zz

    def zto(k):
        return lax.rem(z + OFFS[k], Z)

    def zfrom(k):
        return lax.rem(z + Z - OFFS[k], Z)

    def remote(src, dst, ss, rs, dev):
        return pltpu.make_async_remote_copy(
            src_ref=src, dst_ref=dst, send_sem=ss, recv_sem=rs, device_id=dev, device_id_type=MESH
        )

    def loads(r):
        base = jnp.minimum(GV * lax.rem(y + r, Y), VARS - GV)
        lons = pl.ds(0, 45)
        every = [
            pltpu.make_async_copy(n.at[pl.ds(base, GV)], nbuf.at[r, :, lons], isem.at[r, 0]),
            pltpu.make_async_copy(t.at[pl.ds(base, GV)], tbuf.at[r, :, lons], isem.at[r, 1]),
        ]
        for l in range(LEADS):
            every.append(
                pltpu.make_async_copy(p.at[l, pl.ds(base, GV)], pbuf.at[r, l, :, lons], isem.at[r, 2 + l])
            )
        return every

    order = (2, 1, 3, 0)
    for r in order:
        for c in loads(r):
            c.start()

    barrier = pltpu.get_barrier_semaphore()
    for d in range(1, Y * Z):
        pl.semaphore_signal(barrier, inc=1, device_id=(lat, lax.rem(j + d, Y * Z)), device_id_type=MESH)
    for d in range(1, nlat):
        pl.semaphore_signal(barrier, inc=1, device_id=(lax.rem(lat + d, nlat), j), device_id_type=MESH)

    part[...] = jnp.zeros_like(part)
    first, held = jnp.int32(0), jnp.int32(0)
    for b in range(nlat):
        first = first + jnp.where(b < lat, bands[b], 0)
        held = held + jnp.where(b == lat, bands[b], 0)
    lane = lax.broadcasted_iota(jnp.int32, (1, 128), 1)
    kbuf[40:48] = jnp.zeros((8, 128), jnp.int32)
    kbuf[0:45] = jnp.where(lane < held, flag[...], 0)
    angle = (first + lane).astype(f32) * (math.pi / (NLAT - 1))
    wbuf[...] = jnp.where(lane < held, jnp.sin(angle) * (NLAT / SIN_SUM), 0.0)

    def one(r, iv, b):
        square, offset, product, spread = ([None] * LEADS for _ in range(4))
        truth = None

        def add(total, x):
            return x if total is None else total + x

        for s in range(6):
            rows = pl.ds(8 * s, 8)
            m = kbuf[8 * s : 8 * s + 8] != 0
            nn = nbuf[r, b, rows, :]
            tt = jnp.where(m, tbuf[r, b, rows, :] - nn, 0.0)
            truth = add(truth, tt * tt)
            for l in range(LEADS):
                f = jnp.where(m, pbuf[r, l, b, rows, :] - nn, 0.0)
                e = f - tt
                square[l] = add(square[l], e * e)
                offset[l] = add(offset[l], e)
                product[l] = add(product[l], f * tt)
                spread[l] = add(spread[l], f * f)
        for l in range(LEADS):
            q = iv * LEADS + l
            zd = q // PAIRS
            i = q - zd * PAIRS
            for s, x in enumerate((square[l], offset[l], product[l], spread[l])):
                part[r, zd, pl.ds(s * PAIRS + i, 1), :] = jnp.sum(x, axis=0, keepdims=True)
        tr = jnp.sum(truth, axis=0, keepdims=True)
        for zd in ((iv * LEADS) // PAIRS, (iv * LEADS + LEADS - 1) // PAIRS):
            part[r, zd, pl.ds(4 * PAIRS + iv - (PAIRS * zd) // LEADS, 1), :] = tr

    def compute(r):
        off = GV * lax.rem(y + r, Y) - jnp.minimum(GV * lax.rem(y + r, Y), VARS - GV)
        for c in loads(r):
            c.wait()

        def step(c, carry):
            for u in range(3):
                iv = c * 3 + u
                one(r, iv, iv + off)
            return carry

        lax.fori_loop(0, (GV - off) // 3, step, 0)

    def to_relay(k):
        return remote(part.at[2, zto(k)], rel.at[k], rel_s.at[k], rel_r.at[k], (lat, at(up if k % 2 == 0 else down, z)))

    def direct(k):
        if k % 2:
            return remote(part.at[1, zto(k)], in_m.at[k], dir_s.at[k], m_r.at[k], (lat, at(up, z)))
        return remote(part.at[3, zto(k)], in_p.at[k], dir_s.at[k], p_r.at[k], (lat, at(down, z)))

    def relayed(k):
        if k % 2:
            return remote(part.at[3, zto(k)], in_p.at[k], fwd_s.at[k], p_r.at[k], (lat, at(down, z)))
        return remote(part.at[1, zto(k)], in_m.at[k], fwd_s.at[k], m_r.at[k], (lat, at(up, z)))

    def along_z(k):
        return remote(part.at[0, zto(k)], zin.at[k], z_s.at[k], z_r.at[k], (lat, at(y, zto(k))))

    compute(2)
    pl.semaphore_wait(barrier, Y * Z - 1 + nlat - 1)
    for k in range(Z):
        to_relay(k).start()
    compute(1)
    for k in range(1, Z, 2):
        direct(k).start()
    compute(3)
    for k in range(0, Z, 2):
        direct(k).start()
    compute(0)
    for k in range(Z):
        to_relay(k).wait_recv()
        r = 3 if k % 2 else 1
        part[r, zto(k)] = part[r, zto(k)] + rel[k]
        relayed(k).start()

    def from_y(k):
        a, b = (direct(k), relayed(k)) if k % 2 else (relayed(k), direct(k))
        a.wait_recv()
        b.wait_recv()
        return part[0, zto(k)] + (in_m[k] + in_p[k])

    for k in range(Z - 1):
        part[0, zto(k)] = from_y(k)
        along_z(k).start()
    s = from_y(Z - 1)
    for k in range(Z - 1):
        along_z(k).wait_recv()
        s = s + zin[k]

    c = 1.0 / NLON
    pair = lax.broadcasted_iota(jnp.int32, (PAIRS, 128), 0) + lax.rem(j, 4)
    sbuf[0:ROWS] = s
    square, offset = sbuf[0:9], sbuf[9:18]
    product, spread = sbuf[18:27], sbuf[27:36]
    truth = jnp.where(pair < 4, sbuf[36:37], jnp.where(pair < 8, sbuf[37:38], sbuf[38:39]))
    gath[j, 0:9] = square * c
    gath[j, 9:18] = offset * c
    gath[j, 18:27] = (product * c) / jnp.sqrt(jnp.maximum(spread * c, FLOOR) * jnp.maximum(truth * c, FLOOR))

    def spread_z(k, owner):
        return remote(gath.at[owner], gath.at[owner], a_s.at[k], a_r.at[k], (lat, at(y, zto(k))))

    def to_up(k, owner):
        return remote(gath.at[owner], gath.at[owner], ym_s.at[k], ym_r.at[k], (lat, at(up, z)))

    def to_down(k, owner):
        return remote(gath.at[owner], gath.at[owner], yp_s.at[k], yp_r.at[k], (lat, at(down, z)))

    def onward(k, owner):
        return remote(gath.at[owner], gath.at[owner], opp_s.at[k], opp_r.at[k], (lat, at(down if k % 2 else up, z)))

    for k in range(Z - 1):
        spread_z(k, j).start()
    to_up(Z - 1, j).start()
    to_down(Z - 1, j).start()

    sbuf[36:45] = truth
    sbuf[45:48] = jnp.zeros((3, 128), f32)
    column = jnp.sum(sbuf[...] * wbuf[...], axis=1, keepdims=True)
    here = lax.broadcasted_iota(jnp.int32, (48, 128), 0) == lax.broadcasted_iota(jnp.int32, (48, 128), 1)
    lin[lat] = jnp.sum(jnp.where(here, column, 0.0), axis=0, keepdims=True)

    def to_band(d):
        return remote(lin.at[lat], lin.at[lat], l_s.at[d], l_r.at[d], (lax.rem(lat + d, nlat), j))

    def from_band(d):
        src = lax.rem(lat + nlat - d, nlat)
        return remote(lin.at[src], lin.at[src], l_s.at[d], l_r.at[d], (lax.rem(lat + d, nlat), j))

    def to_all(d):
        return remote(hall.at[j], hall.at[j], h_s.at[d], h_r.at[d], (lat, lax.rem(j + d, Y * Z)))

    def from_all(d):
        src = lax.rem(j + Y * Z - d, Y * Z)
        return remote(hall.at[src], hall.at[src], h_s.at[d], h_r.at[d], (lat, lax.rem(j + d, Y * Z)))

    for d in range(1, nlat):
        to_band(d).start()
    for d in range(1, nlat):
        from_band(d).wait_recv()
    total = lin[0]
    for b in range(1, nlat):
        total = total + lin[b]
    total = total * (1.0 / (NLAT * NLON))
    over = pltpu.roll(total, 128 - 9, 1)
    under = pltpu.roll(total, 128 - 18, 1)
    skill = total / jnp.sqrt(jnp.maximum(over, FLOOR) * jnp.maximum(under, FLOOR))
    measures = jnp.where(lane < 9, jnp.sqrt(jnp.maximum(total, FLOOR)), jnp.where(lane < 18, total, skill))
    hall[j] = jnp.where(lane < SCORES, measures, 0.0)
    for d in range(1, Y * Z):
        to_all(d).start()

    for k in range(Z - 1):
        owner = at(y, zfrom(k))
        spread_z(k, owner).wait_recv()
        to_up(k, owner).start()
        to_down(k, owner).start()
    for k in (7, 0, 1, 2, 3, 4, 5, 6):
        below, above = at(down, zfrom(k)), at(up, zfrom(k))
        to_up(k, below).wait_recv()
        to_down(k, above).wait_recv()
        onward(k, above if k % 2 else below).start()
    opposite = lax.rem(y + 2, Y)
    for k in range(Z):
        onward(k, at(opposite, zfrom(k))).wait_recv()

    def place(c, pairs):
        for a in range(4):
            for i in range(PAIRS):
                q = a * PAIRS + i
                if q < pairs:
                    for m, o in enumerate((o0, o1, o2)):
                        o[q % LEADS, pl.ds(c * PAIRS + q // LEADS, 1), :] = gath[4 * c + a, m * PAIRS + i : m * PAIRS + i + 1]

    def placed(c, carry):
        place(c, 36)
        return carry

    lax.fori_loop(0, 7, placed, 0)
    place(7, LEADS * VARS - 7 * 36)

    for d in range(1, Y * Z):
        from_all(d).wait_recv()
    table = hall[:, 0, :]
    owner = lax.broadcasted_iota(jnp.int32, (Y * Z, 128), 0)
    var = lax.broadcasted_iota(jnp.int32, (Y * Z, 128), 1)
    for l in range(LEADS):
        q = var * LEADS + l
        mine = lax.shift_right_logical(q * 7282, 16)
        chosen = jnp.where(mine == owner, 1.0, 0.0)
        picked = lax.dot_general(
            table, chosen, (((0,), (0,)), ((), ())), precision=lax.Precision.HIGHEST, preferred_element_type=f32
        )[0:32]
        rest = q - mine * PAIRS
        for m, g in enumerate((g0, g1, g2)):
            line = jnp.sum(jnp.where(owner == rest + m * PAIRS, picked, 0.0), axis=0, keepdims=True)
            g[l : l + 1, :] = line[:, 0:VARS]

    for k in range(Z):
        to_relay(k).wait_send()
        direct(k).wait_send()
        relayed(k).wait_send()
        to_up(k, j).wait_send()
        to_down(k, j).wait_send()
        onward(k, j).wait_send()
    for k in range(Z - 1):
        along_z(k).wait_send()
        spread_z(k, j).wait_send()
    for d in range(1, nlat):
        to_band(d).wait_send()
    for d in range(1, Y * Z):
        to_all(d).wait_send()


def local(prediction_fields, verifying_state, normal_state, evaluated_point_flag, parallels_each_strip):
    f32 = jnp.float32
    hbm, vmem, smem = (pl.BlockSpec(memory_space=m) for m in (pltpu.HBM, pltpu.VMEM, pltpu.SMEM))
    dma = pltpu.SemaphoreType.DMA
    block = (Z, ROWS, 128)
    return pl.pallas_call(
        kernel,
        out_shape=[jax.ShapeDtypeStruct((LEADS, VARS, 128), f32)] * 3 + [jax.ShapeDtypeStruct((LEADS, VARS), f32)] * 3,
        in_specs=[hbm, hbm, hbm, vmem, smem],
        out_specs=[vmem] * 6,
        scratch_shapes=[
            pltpu.VMEM((Y, LEADS, GV, 48, 128), f32),
            pltpu.VMEM((Y, GV, 48, 128), f32),
            pltpu.VMEM((Y, GV, 48, 128), f32),
            pltpu.VMEM((48, 128), jnp.int32),
            pltpu.VMEM((1, 128), f32),
            pltpu.VMEM((Y, *block), f32),
            pltpu.VMEM(block, f32),
            pltpu.VMEM(block, f32),
            pltpu.VMEM(block, f32),
            pltpu.VMEM((Z - 1, ROWS, 128), f32),
            pltpu.VMEM((48, 128), f32),
            pltpu.VMEM((Y * Z, SCORES, 128), f32),
            pltpu.VMEM((8, 1, 128), f32),
            pltpu.VMEM((Y * Z, 1, 128), f32),
            dma((Y, 6)),
            *[dma((Z,))] * 16,
            *[dma((8,))] * 2,
            *[dma((Y * Z,))] * 2,
        ],
        compiler_params=pltpu.CompilerParams(
            collective_id=0, has_side_effects=True, vmem_limit_bytes=48 * 1024 * 1024
        ),
    )(prediction_fields, verifying_state, normal_state, evaluated_point_flag, parallels_each_strip)


def solution(mesh):
    placed = (P(None, None, "lon", "lat"), P(None, "lon", "lat"), P(None, "lon", "lat"), P("lon", "lat"), P())
    return jax.shard_map(
        local,
        mesh=mesh,
        in_specs=placed,
        out_specs=(P(None, None, "lat"), P(None, None, "lat"), P(None, None, "lat"), P(), P(), P()),
        check_vma=False,
    )
```

time: 131 us -> 50 us (0.38)
  blocking collectives: 86.8 us -> 0 us
  Pallas kernels: 0 us -> 37.5 us
  other arithmetic: 16.4 us -> 0 us
  starting transfers between devices: 11.5 us -> 0 us
  local copies, waits for them, and re-layouts: 13.6 us -> 11.3 us
    all_gather x1 -> x0, blocking collectives: 47.5 us -> none  [gather_turned(): filled, at, done = (lax.all_gather(both, axis, axis=0, tiled=True), 0, [])]
    psum x4 -> x0, blocking collectives: 39.2 us -> none  [by_axis(): return functools.reduce(lax.psum, axes, shard)]
    pallas_call x0 -> x1, Pallas kernels: none -> 37.5 us  [local(): pl.pallas_call(kernel, out_shape=[jax.ShapeDtypeStruct((LEADS, VARS, 128)...]
    reduce_sum x6 -> x0, other arithmetic: 12.8 us -> none  [the longest x1 10.2 us: local(): jnp.sum(retained_entries * predicted_anomaly * observed_anomaly[None], ax...]
    all_to_all x1 -> x0, starting transfers between devices: 11.5 us -> none  [sent_and_summed(): lax.all_to_all(split_up(shard, dim, devices), axis, 0, 0, tiled=True)]
    concatenate x6 -> x0, local copies, waits for them, and re-layouts: 3.03 us -> none  [local(): jnp.concatenate([jnp.sum(retained_entries * mistake_field * mistake_field...]
    unnamed x13 -> x12, local copies, waits for them, and re-layouts: 6.8 us -> 9.2 us
    pallas_call x0 -> x3, local copies, waits for them, and re-layouts: none -> 2.09 us  [local(): pl.pallas_call(kernel, out_shape=[jax.ShapeDtypeStruct((LEADS, VARS, 128)...]
  transfers between devices with their start and end apart: 1 -> 0, of which waited for: 0 -> 0; matrix products, arithmetic and copies ran while one was open for 5% -> 0% of each run, Pallas kernels for 0% -> 0%
where the time goes in v1:
time: 50 us; the launch traced here: 49.4 us
  Pallas kernels  37.5 us (75%)
  local copies, waits for them, and re-layouts  11.3 us (23%)
  between operations  0.68 us (1%)
    pallas_call x1, Pallas kernels, local(): pl.pallas_call(kernel, out_shape=[jax.ShapeDtypeStruct((LEADS, VARS, 128)...  37.5 us
    unnamed x12, local copies, waits for them, and re-layouts  9.2 us
    pallas_call x3, local copies, waits for them, and re-layouts, local(): pl.pallas_call(kernel, out_shape=[jax.ShapeDtypeStruct((LEADS, VARS, 128)...  2.09 us

profile of v1, /device:TPU:2, one launch (start us, length us, event | category | flops | bytes accessed | tf_op | source)
XLA Modules:
  0.0 49.4 jit_solution(5110667636391631594)
XLA Ops:
  0.6 0.0 copy-start.2
  0.6 1.9 %copy.12.t = f32[69,45,128]{2,1,0:T(8,128)S(1)} copy(f32[69,45,128]{2,0,1:T(8,128)} %param.6) | data formatting | bytes 3179520 | tf_op args[1]
  2.6 2.2 %copy.13.n = f32[69,45,128]{2,1,0:T(8,128)S(1)} copy(f32[69,45,128]{2,0,1:T(8,128)} %param.7) | data formatting | bytes 3179520 | tf_op args[2]
  4.7 0.0 copy-done.2
  4.7 0.0 copy-start
  4.8 0.0 copy-start.1
  4.8 3.4 %copy.11.p = f32[4,69,45,128]{3,2,1,0:T(8,128)} copy(f32[4,69,45,128]{3,0,2,1:T(4,128)S(1)} %copy-done.2) | data formatting | bytes 12718080 | tf_op args[0]
  8.1 0.0 copy-done
  8.1 0.0 copy-done.1
  8.1 37.5 %shard_map.100 = (f32[4,69,128]{2,1,0:T(8,128)S(1)}, f32[4,69,128]{2,1,0:T(8,128)S(1)}, f32[4,69,128]{2,1,0:T(8,128)S(1)}, f32[4,69]{1,0:T(4,128)S(1)}, f32[4,69]{1,0:T(4,128)S(1)}, /*index=5*/f32[4,69]{1,0:T(4,128)S(1)}) custom-call(f32[4,69,45,128]{3,2,1,0:T(8,128)} %copy.11.p, f32[69,45,128]{2,1,0:T(8,128)S(1)} %copy.12.t, f32[69,45,128]{2,1,0:T(8,128)S(1)} %copy.13.n, ...), custom_call_target="tpu_custom_call" | custom-call | tf_op jit(solution)/shard_map/pallas_call | solution.py:303
  45.6 0.7 %copy.14 = f32[4,69,128]{2,0,1:T(4,128)} copy(f32[4,69,128]{2,1,0:T(8,128)S(1)} %get-tuple-element.6) | data formatting | bytes 282624 | tf_op jit(solution)/shard_map/pallas_call | solution.py:303
  46.3 0.7 %copy.15 = f32[4,69,128]{2,0,1:T(4,128)} copy(f32[4,69,128]{2,1,0:T(8,128)S(1)} %get-tuple-element.7) | data formatting | bytes 282624 | tf_op jit(solution)/shard_map/pallas_call | solution.py:303
  47.0 0.7 %copy.16 = f32[4,69,128]{2,0,1:T(4,128)} copy(f32[4,69,128]{2,1,0:T(8,128)S(1)} %get-tuple-element.8) | data formatting | bytes 282624 | tf_op jit(solution)/shard_map/pallas_call | solution.py:303
  47.7 0.6 %copy.20 = f32[4,69]{1,0:T(4,128)} copy(f32[4,69]{1,0:T(4,128)S(1)} %get-tuple-element.21) | data formatting | bytes 2208
  48.3 0.6 %copy.21 = f32[4,69]{1,0:T(4,128)} copy(f32[4,69]{1,0:T(4,128)S(1)} %get-tuple-element.22) | data formatting | bytes 2208
  48.9 0.6 %copy.22 = f32[4,69]{1,0:T(4,128)} copy(f32[4,69]{1,0:T(4,128)S(1)} %get-tuple-element.23) | data formatting | bytes 2208
Async XLA Ops:
  0.6 4.1 %copy-start.2 = (f32[4,69,45,128]{3,0,2,1:T(4,128)S(1)}, f32[4,69,45,128]{3,0,2,1:T(4,128)}, u32[]{:S(2)}) copy-start(f32[4,69,45,128]{3,0,2,1:T(4,128)} %param.5) | copy-start | bytes 19077124
  4.7 3.4 %copy-start = (s32[45,128]{1,0:T(8,128)S(1)}, s32[45,128]{1,0:T(8,128)}, u32[]{:S(2)}) copy-start(s32[45,128]{1,0:T(8,128)} %flag.1) | copy-start | bytes 69124
  4.8 3.4 %copy-start.1 = (s32[8]{0:T(128)S(1)}, s32[8]{0:T(128)}, u32[]{:S(2)}) copy-start(s32[8]{0:T(128)} %bands.1) | copy-start | bytes 100

commit v2 on v1

v2 whole, which is shorter than its diff:
```python
import math

import jax
import jax.numpy as jnp
from jax import lax
from jax.experimental import pallas as pl
from jax.experimental.pallas import tpu as pltpu
from jax.sharding import PartitionSpec as P

MESH = pl.DeviceIdType.MESH
Y, Z = 4, 8
LEADS, VARS, LONS = 4, 69, 45
GV = 18
PAIRS = 9
PADDED = Y * Z * PAIRS
ROWS = 4 * PAIRS + 3
SCORES = 3 * PAIRS
TILES = 9
OFFS = (4, 3, 5, 2, 6, 1, 7, 0)
NLAT, NLON = 721, 1440
FLOOR = 0.1
SIN_SUM = sum(math.sin(math.pi * g / (NLAT - 1)) for g in range(NLAT))


def kernel(p, t, n, flag, bands, gath, g0, g1, g2,
           pbuf, tbuf, nbuf, kbuf, wbuf, part, ptru, rel, rel_t, in_m, in_mt, in_p, in_pt, tsum, zout, zin, sbuf, lin, hall,
           psem, tnsem, rel_s, rel_r, dir_s, fwd_s, m_r, p_r, z_s, z_r, a_s, a_r, ym_s, yp_s, ym_r, yp_r,
           opp_s, opp_r, l_s, l_r, h_s, h_r):
    lat, j = lax.axis_index("lat"), lax.axis_index("lon")
    nlat = 8
    y, z = j // Z, lax.rem(j, Z)
    up, down, opposite = (lax.rem(y + r, Y) for r in (1, Y - 1, 2))
    f32 = jnp.float32

    def at(yy, zz):
        return yy * Z + zz

    def zto(k):
        return lax.rem(z + OFFS[k], Z)

    def zfrom(k):
        return lax.rem(z + Z - OFFS[k], Z)

    def remote(src, dst, ss, rs, dev):
        return pltpu.make_async_remote_copy(
            src_ref=src, dst_ref=dst, send_sem=ss, recv_sem=rs, device_id=dev, device_id_type=MESH
        )

    def load_p(tile):
        return pltpu.make_async_copy(p.at[pl.ds(jnp.minimum(8 * tile, VARS - 8), 8)], pbuf.at[tile], psem.at[tile])

    def load_tn(c):
        lons, rows = pl.ds(9 * c, 9), pl.ds(0, VARS)
        return (
            pltpu.make_async_copy(n.at[lons], nbuf.at[lons, rows], tnsem.at[c, 0]),
            pltpu.make_async_copy(t.at[lons], tbuf.at[lons, rows], tnsem.at[c, 1]),
        )

    wrap_up, wrap_down = opposite == 0, opposite == Y - 1
    phases = (
        (2 * opposite, 3),
        (jnp.where(wrap_up, 6, 2 * opposite - 2), jnp.where(wrap_up, 3, 2)),
        (jnp.where(wrap_down, 0, 2 * opposite + 3), jnp.where(wrap_down, 3, 2)),
        (
            jnp.where(wrap_up, 5, jnp.where(opposite == 1, 7, jnp.where(opposite == 2, 0, 3))),
            jnp.where(wrap_up | wrap_down, 1, 2),
        ),
    )

    def start_p(phase):
        first, count = phases[phase]

        def go(i, carry):
            load_p(first + i).start()
            return carry

        lax.fori_loop(0, count, go, 0)

    for c in range(5):
        for d in load_tn(c):
            d.start()
        if c == 0:
            start_p(0)
    for phase in (1, 2, 3):
        start_p(phase)

    barrier = pltpu.get_barrier_semaphore()
    for d in range(1, Y * Z):
        pl.semaphore_signal(barrier, inc=1, device_id=(lat, lax.rem(j + d, Y * Z)), device_id_type=MESH)
    for d in range(1, nlat):
        pl.semaphore_signal(barrier, inc=1, device_id=(lax.rem(lat + d, nlat), j), device_id_type=MESH)

    part[:, LEADS * VARS : PADDED] = jnp.zeros((4, PADDED - LEADS * VARS, 128), f32)
    ptru[VARS : Y * GV] = jnp.zeros((Y * GV - VARS, 128), f32)
    first, held = jnp.int32(0), jnp.int32(0)
    for b in range(nlat):
        first = first + jnp.where(b < lat, bands[b], 0)
        held = held + jnp.where(b == lat, bands[b], 0)
    lane = lax.broadcasted_iota(jnp.int32, (1, 128), 1)
    for lon in range(LONS):
        kbuf[lon] = jnp.broadcast_to(jnp.where(lane < held, flag[lon : lon + 1], 0), (8, 128))
    angle = (first + lane).astype(f32) * (math.pi / (NLAT - 1))
    wbuf[...] = jnp.where(lane < held, jnp.sin(angle) * (NLAT / SIN_SUM), 0.0)

    prows = pbuf.reshape(TILES * 8 * LONS * LEADS, 128)

    def sums(tile):
        top = jnp.minimum(8 * tile, VARS - 8)
        base = tile * (8 * LONS * LEADS)

        def column(lon, totals):
            m = kbuf[lon] != 0
            nn = nbuf[lon, pl.ds(top, 8), :]
            tt = jnp.where(m, tbuf[lon, pl.ds(top, 8), :] - nn, 0.0)
            new = [totals[0] + tt * tt]
            for l in range(LEADS):
                square, offset, product, spread = totals[1 + 4 * l : 5 + 4 * l]
                f = jnp.where(m, prows[pl.ds(base + lon * LEADS + l, 8, stride=LONS * LEADS), :] - nn, 0.0)
                e = f - tt
                new += [square + e * e, offset + e, product + f * tt, spread + f * f]
            return tuple(new)

        def columns(c, totals):
            for u in range(9):
                totals = column(9 * c + u, totals)
            return totals

        totals = lax.fori_loop(0, 5, columns, (jnp.zeros((8, 128), f32),) * 17)
        ptru[pl.ds(top, 8), :] = totals[0]
        for l in range(LEADS):
            for s in range(4):
                part[s, pl.ds(top * LEADS + l, 8, stride=LEADS), :] = totals[1 + 4 * l + s]

    def compute(phase):
        first, count = phases[phase]

        def go(i, carry):
            load_p(first + i).wait()
            sums(first + i)
            return carry

        lax.fori_loop(0, count, go, 0)

    def block(g, k):
        return part.at[:, pl.ds(PAIRS * at(g, zto(k)), PAIRS), :]

    def group(g):
        return ptru.at[pl.ds(GV * g, GV), :]

    def take(g, k):
        return part[:, pl.ds(PAIRS * at(g, zto(k)), PAIRS), :]

    def to_relay(k):
        dev = (lat, at(down if k % 2 else up, z))
        if k == Z:
            return remote(group(opposite), rel_t, rel_s.at[k], rel_r.at[k], dev)
        return remote(block(opposite, k), rel.at[k], rel_s.at[k], rel_r.at[k], dev)

    def upwards(k, sems):
        dev = (lat, at(up, z))
        if k == Z:
            return remote(group(up), in_mt, sems.at[k], m_r.at[k], dev)
        return remote(block(up, k), in_m.at[k], sems.at[k], m_r.at[k], dev)

    def downwards(k, sems):
        dev = (lat, at(down, z))
        if k == Z:
            return remote(group(down), in_pt, sems.at[k], p_r.at[k], dev)
        return remote(block(down, k), in_p.at[k], sems.at[k], p_r.at[k], dev)

    def direct(k):
        return (upwards if k % 2 else downwards)(k, dir_s)

    def relayed(k):
        return (downwards if k % 2 else upwards)(k, fwd_s)

    def along_z(k):
        return remote(zout.at[k], zin.at[k], z_s.at[k], z_r.at[k], (lat, at(y, zto(k))))

    each = (Z, *range(Z))
    with jax.named_scope("load_tn"):
        for c in range(5):
            for d in load_tn(c):
                d.wait()
    with jax.named_scope("compute_a"):
        compute(0)
    with jax.named_scope("barrier"):
        pl.semaphore_wait(barrier, Y * Z - 1 + nlat - 1)
    for k in each:
        to_relay(k).start()
    with jax.named_scope("compute_b"):
        compute(1)
    for k in range(1, Z, 2):
        direct(k).start()
    with jax.named_scope("compute_c"):
        compute(2)
    for k in (Z, *range(0, Z, 2)):
        direct(k).start()
    with jax.named_scope("compute_d"):
        compute(3)
    for k in each:
        with jax.named_scope(f"relay#k={k}"):
            to_relay(k).wait_recv()
            g = down if k % 2 else up
            if k == Z:
                ptru[pl.ds(GV * g, GV), :] = ptru[pl.ds(GV * g, GV), :] + rel_t[...]
            else:
                part[:, pl.ds(PAIRS * at(g, zto(k)), PAIRS), :] = take(g, k) + rel[k]
            relayed(k).start()

    def arrived(k):
        upwards(k, dir_s if k % 2 else fwd_s).wait_recv()
        downwards(k, fwd_s if k % 2 else dir_s).wait_recv()

    arrived(Z)
    tsum[...] = ptru[pl.ds(GV * y, GV), :] + (in_mt[...] + in_pt[...])

    def summed(k, out):
        arrived(k)
        x = take(y, k) + (in_m[k] + in_p[k])
        for s in range(4):
            out[PAIRS * s : PAIRS * (s + 1)] = x[s]
        out[4 * PAIRS : ROWS] = tsum[pl.ds((PAIRS * zto(k)) // LEADS, 3), :]

    for k in range(Z - 1):
        with jax.named_scope(f"sum_y#k={k}"):
            summed(k, zout.at[k])
            along_z(k).start()
    summed(Z - 1, sbuf)
    s = sbuf[0:ROWS]
    for k in range(Z - 1):
        with jax.named_scope(f"sum_z#k={k}"):
            along_z(k).wait_recv()
            s = s + zin[k]

    c = 1.0 / NLON
    pair = lax.broadcasted_iota(jnp.int32, (PAIRS, 128), 0) + lax.rem(j, 4)
    sbuf[0:ROWS] = s
    square, offset = sbuf[0:9], sbuf[9:18]
    product, spread = sbuf[18:27], sbuf[27:36]
    truth = jnp.where(pair < 4, sbuf[36:37], jnp.where(pair < 8, sbuf[37:38], sbuf[38:39]))
    mine = pl.ds(PAIRS * j, PAIRS)
    gath[0, mine, :] = square * c
    gath[1, mine, :] = offset * c
    gath[2, mine, :] = (product * c) / jnp.sqrt(jnp.maximum(spread * c, FLOOR) * jnp.maximum(truth * c, FLOOR))

    def scores(owner):
        return gath.at[:, pl.ds(PAIRS * owner, PAIRS), :]

    def spread_z(k, owner):
        return remote(scores(owner), scores(owner), a_s.at[k], a_r.at[k], (lat, at(y, zto(k))))

    def to_up(k, owner):
        return remote(scores(owner), scores(owner), ym_s.at[k], ym_r.at[k], (lat, at(up, z)))

    def to_down(k, owner):
        return remote(scores(owner), scores(owner), yp_s.at[k], yp_r.at[k], (lat, at(down, z)))

    def onward(k, owner):
        return remote(scores(owner), scores(owner), opp_s.at[k], opp_r.at[k], (lat, at(down if k % 2 else up, z)))

    for k in range(Z - 1):
        spread_z(k, j).start()
    to_up(Z - 1, j).start()
    to_down(Z - 1, j).start()

    sbuf[36:45] = truth
    sbuf[45:48] = jnp.zeros((3, 128), f32)
    column = jnp.sum(sbuf[...] * wbuf[...], axis=1, keepdims=True)
    here = lax.broadcasted_iota(jnp.int32, (48, 128), 0) == lax.broadcasted_iota(jnp.int32, (48, 128), 1)
    lin[lat] = jnp.sum(jnp.where(here, column, 0.0), axis=0, keepdims=True)

    def to_band(d):
        return remote(lin.at[lat], lin.at[lat], l_s.at[d], l_r.at[d], (lax.rem(lat + d, nlat), j))

    def from_band(d):
        src = lax.rem(lat + nlat - d, nlat)
        return remote(lin.at[src], lin.at[src], l_s.at[d], l_r.at[d], (lax.rem(lat + d, nlat), j))

    def to_all(d):
        return remote(hall.at[j], hall.at[j], h_s.at[d], h_r.at[d], (lat, lax.rem(j + d, Y * Z)))

    def from_all(d):
        src = lax.rem(j + Y * Z - d, Y * Z)
        return remote(hall.at[src], hall.at[src], h_s.at[d], h_r.at[d], (lat, lax.rem(j + d, Y * Z)))

    for d in range(1, nlat):
        to_band(d).start()
    with jax.named_scope("bands"):
        for d in range(1, nlat):
            from_band(d).wait_recv()
    total = lin[0]
    for b in range(1, nlat):
        total = total + lin[b]
    total = total * (1.0 / (NLAT * NLON))
    over = pltpu.roll(total, 128 - 9, 1)
    under = pltpu.roll(total, 128 - 18, 1)
    skill = total / jnp.sqrt(jnp.maximum(over, FLOOR) * jnp.maximum(under, FLOOR))
    measures = jnp.where(lane < 9, jnp.sqrt(jnp.maximum(total, FLOOR)), jnp.where(lane < 18, total, skill))
    hall[j] = jnp.where(lane < SCORES, measures, 0.0)
    for d in range(1, Y * Z):
        to_all(d).start()

    for k in range(Z - 1):
        with jax.named_scope(f"gather_z#k={k}"):
            owner = at(y, zfrom(k))
            spread_z(k, owner).wait_recv()
            to_up(k, owner).start()
            to_down(k, owner).start()
    for k in (7, 0, 1, 2, 3, 4, 5, 6):
        with jax.named_scope(f"gather_y#k={k}"):
            below, above = at(down, zfrom(k)), at(up, zfrom(k))
            to_up(k, below).wait_recv()
            to_down(k, above).wait_recv()
            onward(k, above if k % 2 else below).start()
    for k in range(Z):
        with jax.named_scope(f"gather_o#k={k}"):
            onward(k, at(opposite, zfrom(k))).wait_recv()

    with jax.named_scope("globals"):
        for d in range(1, Y * Z):
            from_all(d).wait_recv()
    table = hall[:, 0, :]
    owner = lax.broadcasted_iota(jnp.int32, (Y * Z, 128), 0)
    var = lax.broadcasted_iota(jnp.int32, (Y * Z, 128), 1)
    for l in range(LEADS):
        q = var * LEADS + l
        mine = lax.shift_right_logical(q * 7282, 16)
        chosen = jnp.where(mine == owner, 1.0, 0.0)
        picked = lax.dot_general(
            table, chosen, (((0,), (0,)), ((), ())), precision=lax.Precision.HIGHEST, preferred_element_type=f32
        )[0:32]
        rest = q - mine * PAIRS
        for m, g in enumerate((g0, g1, g2)):
            line = jnp.sum(jnp.where(owner == rest + m * PAIRS, picked, 0.0), axis=0, keepdims=True)
            g[l : l + 1, :] = line[:, 0:VARS]

    for k in each:
        to_relay(k).wait_send()
        direct(k).wait_send()
        relayed(k).wait_send()
    for k in range(Z):
        to_up(k, j).wait_send()
        to_down(k, j).wait_send()
        onward(k, j).wait_send()
    for k in range(Z - 1):
        along_z(k).wait_send()
        spread_z(k, j).wait_send()
    for d in range(1, nlat):
        to_band(d).wait_send()
    for d in range(1, Y * Z):
        to_all(d).wait_send()


def writer(gath, s0, s1, s2, o0, o1, o2, g0, g1, g2, sems):
    rows = LEADS * VARS
    copies = [
        pltpu.make_async_copy(gath.at[m, pl.ds(0, rows)], o.reshape(rows, 128), sems.at[m])
        for m, o in enumerate((o0, o1, o2))
    ]
    copies += [
        pltpu.make_async_copy(s, g, sems.at[3 + m]) for m, (s, g) in enumerate(((s0, g0), (s1, g1), (s2, g2)))
    ]
    for c in copies:
        c.start()
    for c in copies:
        c.wait()


def local(prediction_fields, verifying_state, normal_state, evaluated_point_flag, parallels_each_strip):
    f32 = jnp.float32
    hbm, vmem, smem = (pl.BlockSpec(memory_space=m) for m in (pltpu.HBM, pltpu.VMEM, pltpu.SMEM))
    dma = pltpu.SemaphoreType.DMA
    single = [jax.ShapeDtypeStruct((LEADS, VARS), f32)] * 3
    gathered, *means = pl.pallas_call(
        kernel,
        out_shape=[jax.ShapeDtypeStruct((3, PADDED, 128), f32)] + single,
        in_specs=[hbm, hbm, hbm, vmem, smem],
        out_specs=[vmem] * 4,
        scratch_shapes=[
            pltpu.VMEM((TILES, 8, LONS, LEADS, 128), f32),
            pltpu.VMEM((LONS, 72, 128), f32),
            pltpu.VMEM((LONS, 72, 128), f32),
            pltpu.VMEM((LONS, 8, 128), jnp.int32),
            pltpu.VMEM((1, 128), f32),
            pltpu.VMEM((4, PADDED, 128), f32),
            pltpu.VMEM((Y * GV, 128), f32),
            *[pltpu.VMEM((Z, 4, PAIRS, 128), f32), pltpu.VMEM((GV, 128), f32)] * 3,
            pltpu.VMEM((GV, 128), f32),
            pltpu.VMEM((Z - 1, ROWS, 128), f32),
            pltpu.VMEM((Z - 1, ROWS, 128), f32),
            pltpu.VMEM((48, 128), f32),
            pltpu.VMEM((8, 1, 128), f32),
            pltpu.VMEM((Y * Z, 1, 128), f32),
            dma((TILES,)),
            dma((5, 2)),
            *[dma((Z + 1,))] * 6,
            *[dma((Z,))] * 10,
            *[dma((8,))] * 2,
            *[dma((Y * Z,))] * 2,
        ],
        compiler_params=pltpu.CompilerParams(
            collective_id=0, has_side_effects=True, vmem_limit_bytes=53 * 1024 * 1024
        ),
    )(
        jnp.transpose(prediction_fields, (1, 2, 0, 3)),
        jnp.transpose(verifying_state, (1, 0, 2)),
        jnp.transpose(normal_state, (1, 0, 2)),
        evaluated_point_flag,
        parallels_each_strip,
    )
    *zonal, a, b, c = pl.pallas_call(
        writer,
        out_shape=[jax.ShapeDtypeStruct((VARS, LEADS, 128), f32)] * 3 + single,
        in_specs=[vmem] * 4,
        out_specs=[hbm] * 6,
        scratch_shapes=[dma((6,))],
        compiler_params=pltpu.CompilerParams(vmem_limit_bytes=2 * 1024 * 1024),
    )(gathered, *means)
    return (*(jnp.transpose(o, (1, 0, 2)) for o in zonal), a, b, c)


def solution(mesh):
    placed = (P(None, None, "lon", "lat"), P(None, "lon", "lat"), P(None, "lon", "lat"), P("lon", "lat"), P())
    return jax.shard_map(
        local,
        mesh=mesh,
        in_specs=placed,
        out_specs=(P(None, None, "lat"), P(None, None, "lat"), P(None, None, "lat"), P(), P(), P()),
        check_vma=False,
    )
```

time: 50 us -> 40.3 us (0.81)
  local copies, waits for them, and re-layouts: 11.3 us -> 1.39 us
    unnamed x12 -> x4, local copies, waits for them, and re-layouts: 9.2 us -> 1.39 us
    pallas_call x3 -> x0, local copies, waits for them, and re-layouts: 2.09 us -> none  [local(): pl.pallas_call(kernel, out_shape=[jax.ShapeDtypeStruct((LEADS, VARS, 128)...]
    pallas_call x1 -> x2, Pallas kernels: 37.5 us -> 37.7 us  [the longest x1 36.9 us: local(): pl.pallas_call(kernel, out_shape=[jax.ShapeDtypeStruct((3, PADDED, 128),...]
where the time goes in v2:
time: 40.3 us; the launch traced here: 39.7 us
  Pallas kernels  37.7 us (94%)
  local copies, waits for them, and re-layouts  1.39 us (3%)
  between operations  0.65 us (2%)
    pallas_call x1, Pallas kernels, local(): pl.pallas_call(kernel, out_shape=[jax.ShapeDtypeStruct((3, PADDED, 128),...  36.9 us
    unnamed x4, local copies, waits for them, and re-layouts  1.39 us
    pallas_call x1, Pallas kernels, local(): pl.pallas_call(writer, out_shape=[jax.ShapeDtypeStruct((VARS, LEADS, 128)...  0.81 us

profile of v2, /device:TPU:2, one launch (start us, length us, event | category | flops | bytes accessed | tf_op | source)
XLA Modules:
  0.0 39.7 jit_solution(12658071599133371806)
XLA Ops:
  0.6 0.0 copy-start
  0.6 0.7 %copy-done = s32[45,128]{1,0:T(8,128)S(1)} copy-done((s32[45,128]{1,0:T(8,128)S(1)}, s32[45,128]{1,0:T(8,128)}, u32[]{:S(2)}) %copy-start) | copy-done | bytes 23064
  1.4 0.0 copy-start.1
  1.4 0.7 %copy-done.1 = s32[8]{0:T(128)S(1)} copy-done((s32[8]{0:T(128)S(1)}, s32[8]{0:T(128)}, u32[]{:S(2)}) %copy-start.1) | copy-done | bytes 56
  2.0 36.9 %shard_map.100 = (f32[3,288,128]{2,1,0:T(8,128)S(1)}, f32[4,69]{1,0:T(4,128)S(1)}, f32[4,69]{1,0:T(4,128)S(1)}, f32[4,69]{1,0:T(4,128)S(1)}) custom-call(f32[69,45,4,128]{3,2,1,0:T(4,128)} %bitcast.6, f32[45,69,128]{2,1,0:T(8,128)} %bitcast.7, f32[45,69,128]{2,1,0:T(8,128)} %bitcast.8, s32[45,128]{1,0:T(8,128)S(1)} %copy-done, s32[8]{0:T(128)S(1)} %copy-done.1), custom_call_target="tpu_custom_call" | custom-call | tf_op jit(solution)/shard_map/pallas_call | solution.py:375
  38.9 0.8 %shard_map.101 = (f32[69,4,128]{2,1,0:T(4,128)}, f32[69,4,128]{2,1,0:T(4,128)}, f32[69,4,128]{2,1,0:T(4,128)}, f32[4,69]{1,0:T(4,128)}, f32[4,69]{1,0:T(4,128)}, /*index=5*/f32[4,69]{1,0:T(4,128)}) custom-call(f32[3,288,128]{2,1,0:T(8,128)S(1)} %get-tuple-element.16.gath, f32[4,69]{1,0:T(4,128)S(1)} %get-tuple-element.17.s0, ...), custom_call_target="tpu_custom_call" | custom-call | tf_op jit(solution)/shard_map/pallas_call | solution.py:412
Async XLA Ops:
  0.6 0.7 %copy-start = (s32[45,128]{1,0:T(8,128)S(1)}, s32[45,128]{1,0:T(8,128)}, u32[]{:S(2)}) copy-start(s32[45,128]{1,0:T(8,128)} %flag.1) | copy-start | bytes 69124
  1.4 0.7 %copy-start.1 = (s32[8]{0:T(128)S(1)}, s32[8]{0:T(128)}, u32[]{:S(2)}) copy-start(s32[8]{0:T(128)} %bands.1) | copy-start | bytes 100

commit v3 on v2

v3 whole, which is shorter than its diff:
```python
import math

import jax
import jax.numpy as jnp
from jax import lax
from jax.experimental import pallas as pl
from jax.experimental.pallas import tpu as pltpu
from jax.sharding import PartitionSpec as P

MESH = pl.DeviceIdType.MESH
Y, Z = 4, 8
LEADS, VARS, LONS = 4, 69, 45
GV = 18
PAIRS = 9
PADDED = Y * Z * PAIRS
ROWS = 4 * PAIRS + 3
SCORES = 3 * PAIRS
TILES = 9
OFFS = (4, 3, 5, 2, 6, 1, 7, 0)
NLAT, NLON = 721, 1440
FLOOR = 0.1
SIN_SUM = sum(math.sin(math.pi * g / (NLAT - 1)) for g in range(NLAT))


def kernel(p, t, n, flag, bands, gath, g0, g1, g2,
           pbuf, tnbuf, fbuf, brow, kbuf, wbuf, part, ptru, rel, rel_t, in_m, in_mt, in_p, in_pt, tsum, zout, zin, sbuf,
           lin, hall, lsem, fsem, rel_r, fwd_r, a_r, y_r, sent, got):
    lat, j = lax.axis_index("lat"), lax.axis_index("lon")
    nlat = 8
    y, z = j // Z, lax.rem(j, Z)
    up, down, opposite = (lax.rem(y + r, Y) for r in (1, Y - 1, 2))
    f32 = jnp.float32

    def at(yy, zz):
        return yy * Z + zz

    def zto(k):
        return lax.rem(z + OFFS[k], Z)

    def zfrom(k):
        return lax.rem(z + Z - OFFS[k], Z)

    def remote(src, dst, ss, rs, dev):
        return pltpu.make_async_remote_copy(
            src_ref=src, dst_ref=dst, send_sem=ss, recv_sem=rs, device_id=dev, device_id_type=MESH
        )

    def started(ref, sem):
        return pltpu.make_async_copy(ref, ref, sem)

    def load(tile):
        v = pl.ds(jnp.minimum(8 * tile, VARS - 8), 8)
        pltpu.make_async_copy(n.at[:, v], tnbuf.at[tile, 0], lsem.at[0, tile]).start()
        pltpu.make_async_copy(t.at[:, v], tnbuf.at[tile, 1], lsem.at[0, tile]).start()
        pltpu.make_async_copy(p.at[v], pbuf.at[tile], lsem.at[1, tile]).start()

    wrap_up, wrap_down = opposite == 0, opposite == Y - 1
    phases = (
        (2 * opposite, 3),
        (jnp.where(wrap_up, 6, 2 * opposite - 2), jnp.where(wrap_up, 3, 2)),
        (jnp.where(wrap_down, 0, 2 * opposite + 3), jnp.where(wrap_down, 3, 2)),
        (
            jnp.where(wrap_up, 5, jnp.where(opposite == 1, 7, jnp.where(opposite == 2, 0, 3))),
            jnp.where(wrap_up | wrap_down, 1, 2),
        ),
    )

    barrier = pltpu.get_barrier_semaphore()
    for d in range(1, nlat):
        pl.semaphore_signal(barrier, inc=1, device_id=(lax.rem(lat + d, nlat), j), device_id_type=MESH)
    for d in range(1, Y * Z):
        pl.semaphore_signal(barrier, inc=1, device_id=(lat, lax.rem(j + d, Y * Z)), device_id_type=MESH)

    def start_loads(phase):
        first, count = phases[phase]

        def go(i, carry):
            load(first + i)
            return carry

        lax.fori_loop(0, count, go, 0)

    small = (pltpu.make_async_copy(flag, fbuf, fsem.at[0]), pltpu.make_async_copy(bands, brow, fsem.at[1]))
    for d in small:
        d.start()
    for phase in range(4):
        start_loads(phase)

    part[:, LEADS * VARS : PADDED] = jnp.zeros((4, PADDED - LEADS * VARS, 128), f32)
    ptru[VARS : Y * GV] = jnp.zeros((Y * GV - VARS, 128), f32)
    for d in small:
        d.wait()
    first, held = jnp.int32(0), jnp.int32(0)
    for b in range(nlat):
        first = first + jnp.where(b < lat, brow[b], 0)
        held = held + jnp.where(b == lat, brow[b], 0)
    lane = lax.broadcasted_iota(jnp.int32, (1, 128), 1)
    for lon in range(LONS):
        kbuf[lon] = jnp.broadcast_to(jnp.where(lane < held, fbuf[lon : lon + 1], 0), (8, 128))
    angle = (first + lane).astype(f32) * (math.pi / (NLAT - 1))
    wbuf[...] = jnp.where(lane < held, jnp.sin(angle) * (NLAT / SIN_SUM), 0.0)

    prows = pbuf.reshape(TILES * 8 * LONS * LEADS, 128)

    def sums(tile):
        top = jnp.minimum(8 * tile, VARS - 8)
        base = tile * (8 * LONS * LEADS)

        def column(lon, totals):
            m = kbuf[lon] != 0
            nn = tnbuf[tile, 0, lon]
            tt = jnp.where(m, tnbuf[tile, 1, lon] - nn, 0.0)
            new = [totals[0] + tt * tt]
            for l in range(LEADS):
                square, offset, product, spread = totals[1 + 4 * l : 5 + 4 * l]
                f = jnp.where(m, prows[pl.ds(base + lon * LEADS + l, 8, stride=LONS * LEADS), :] - nn, 0.0)
                e = f - tt
                new += [square + e * e, offset + e, product + f * tt, spread + f * f]
            return tuple(new)

        def columns(c, totals):
            for u in range(9):
                totals = column(9 * c + u, totals)
            return totals

        totals = lax.fori_loop(0, 5, columns, (jnp.zeros((8, 128), f32),) * 17)
        ptru[pl.ds(top, 8), :] = totals[0]
        for l in range(LEADS):
            for s in range(4):
                part[s, pl.ds(top * LEADS + l, 8, stride=LEADS), :] = totals[1 + 4 * l + s]

    def compute(phase):
        first, count = phases[phase]

        def go(i, carry):
            started(tnbuf.at[first + i], lsem.at[0, first + i]).wait()
            started(pbuf.at[first + i], lsem.at[1, first + i]).wait()
            sums(first + i)
            return carry

        lax.fori_loop(0, count, go, 0)

    def block(g, k):
        return part.at[:, pl.ds(PAIRS * at(g, zto(k)), PAIRS), :]

    def group(g):
        return ptru.at[pl.ds(GV * g, GV), :]

    def take(g, k):
        return part[:, pl.ds(PAIRS * at(g, zto(k)), PAIRS), :]

    REL, DIR, FWD, TRU, ZS, AS, UPS, DOWNS, OPPS, LS, HS = range(11)
    Z_R, DIR_UP, DIR_DOWN, OPP_R, L_R, H_R, TRU_DOWN = range(7)

    def to_relay(k):
        dev = (lat, at(down if k % 2 else up, z))
        if k == Z:
            return remote(group(opposite), rel_t, sent.at[TRU], rel_r.at[k], dev)
        return remote(block(opposite, k), rel.at[k], sent.at[REL], rel_r.at[k], dev)

    def direct(k):
        if k == Z:
            return remote(group(down), in_pt, sent.at[TRU], got.at[TRU_DOWN], (lat, at(down, z)))
        if k % 2:
            return remote(block(up, k), in_m.at[k], sent.at[DIR], got.at[DIR_UP], (lat, at(up, z)))
        return remote(block(down, k), in_p.at[k], sent.at[DIR], got.at[DIR_DOWN], (lat, at(down, z)))

    def relayed(k):
        if k == Z:
            return remote(group(up), in_mt, sent.at[TRU], fwd_r.at[k], (lat, at(up, z)))
        if k % 2:
            return remote(block(down, k), in_p.at[k], sent.at[FWD], fwd_r.at[k], (lat, at(down, z)))
        return remote(block(up, k), in_m.at[k], sent.at[FWD], fwd_r.at[k], (lat, at(up, z)))

    def along_z(k):
        return remote(zout.at[k], zin.at[k], sent.at[ZS], got.at[Z_R], (lat, at(y, zto(k))))

    each = (Z, *range(Z))
    with jax.named_scope("compute_a"):
        compute(0)
    with jax.named_scope("barrier"):
        pl.semaphore_wait(barrier, Y * Z - 1 + nlat - 1)
    for k in each:
        to_relay(k).start()
    with jax.named_scope("compute_b"):
        compute(1)
    for k in range(1, Z, 2):
        direct(k).start()
    with jax.named_scope("compute_c"):
        compute(2)
    for k in (Z, *range(0, Z, 2)):
        direct(k).start()
    with jax.named_scope("compute_d"):
        compute(3)
    for k in each:
        with jax.named_scope(f"relay#k={k}"):
            to_relay(k).wait_recv()
            g = down if k % 2 else up
            if k == Z:
                ptru[pl.ds(GV * g, GV), :] = ptru[pl.ds(GV * g, GV), :] + rel_t[...]
            else:
                part[:, pl.ds(PAIRS * at(g, zto(k)), PAIRS), :] = take(g, k) + rel[k]
            relayed(k).start()

    direct(Z).wait_recv()
    relayed(Z).wait_recv()
    started(in_m.at[0:4], got.at[DIR_UP]).wait()
    started(in_p.at[0:4], got.at[DIR_DOWN]).wait()
    tsum[...] = ptru[pl.ds(GV * y, GV), :] + (in_mt[...] + in_pt[...])

    def summed(k, out):
        relayed(k).wait_recv()
        x = take(y, k) + (in_m[k] + in_p[k])
        for s in range(4):
            out[PAIRS * s : PAIRS * (s + 1)] = x[s]
        out[4 * PAIRS : ROWS] = tsum[pl.ds((PAIRS * zto(k)) // LEADS, 3), :]

    for k in range(Z - 1):
        with jax.named_scope(f"sum_y#k={k}"):
            summed(k, zout.at[k])
            along_z(k).start()
    summed(Z - 1, sbuf)
    s = sbuf[0:ROWS]
    with jax.named_scope("sum_z"):
        started(zin, got.at[Z_R]).wait()
    for k in range(Z - 1):
        s = s + zin[k]

    c = 1.0 / NLON
    pair = lax.broadcasted_iota(jnp.int32, (PAIRS, 128), 0) + lax.rem(j, 4)
    sbuf[0:ROWS] = s
    square, offset = sbuf[0:9], sbuf[9:18]
    product, spread = sbuf[18:27], sbuf[27:36]
    truth = jnp.where(pair < 4, sbuf[36:37], jnp.where(pair < 8, sbuf[37:38], sbuf[38:39]))
    mine = pl.ds(PAIRS * j, PAIRS)
    gath[0, mine, :] = square * c
    gath[1, mine, :] = offset * c
    gath[2, mine, :] = (product * c) / jnp.sqrt(jnp.maximum(spread * c, FLOOR) * jnp.maximum(truth * c, FLOOR))

    def scores(owner):
        return gath.at[:, pl.ds(PAIRS * owner, PAIRS), :]

    def spread_z(k, owner):
        return remote(scores(owner), scores(owner), sent.at[AS], a_r.at[k], (lat, at(y, zto(k))))

    def to_up(k, owner):
        return remote(scores(owner), scores(owner), sent.at[UPS], y_r.at[k], (lat, at(up, z)))

    def to_down(k, owner):
        return remote(scores(owner), scores(owner), sent.at[DOWNS], y_r.at[k], (lat, at(down, z)))

    def onward(k, owner):
        return remote(scores(owner), scores(owner), sent.at[OPPS], got.at[OPP_R], (lat, at(down if k % 2 else up, z)))

    for k in range(Z - 1):
        spread_z(k, j).start()
    to_up(Z - 1, j).start()
    to_down(Z - 1, j).start()

    sbuf[36:45] = truth
    sbuf[45:48] = jnp.zeros((3, 128), f32)
    column = jnp.sum(sbuf[...] * wbuf[...], axis=1, keepdims=True)
    here = lax.broadcasted_iota(jnp.int32, (48, 128), 0) == lax.broadcasted_iota(jnp.int32, (48, 128), 1)
    lin[lat] = jnp.sum(jnp.where(here, column, 0.0), axis=0, keepdims=True)

    def to_band(d):
        return remote(lin.at[lat], lin.at[lat], sent.at[LS], got.at[L_R], (lax.rem(lat + d, nlat), j))

    def to_all(d):
        return remote(hall.at[j], hall.at[j], sent.at[HS], got.at[H_R], (lat, lax.rem(j + d, Y * Z)))

    for d in range(1, nlat):
        to_band(d).start()
    def from_z(k):
        with jax.named_scope(f"gather_z#k={k}"):
            owner = at(y, zfrom(k))
            spread_z(k, owner).wait_recv()
            to_up(k, owner).start()
            to_down(k, owner).start()

    def from_y(k):
        with jax.named_scope(f"gather_y#k={k}"):
            below, above = at(down, zfrom(k)), at(up, zfrom(k))
            started(gath.at[0, 0 : 2 * SCORES], y_r.at[k]).wait()
            onward(k, above if k % 2 else below).start()

    near = (5, 6, 3, 4, 1, 2, 0)
    for k in near[:2]:
        from_z(k)
    from_y(Z - 1)
    for k in near[2:]:
        from_z(k)
    with jax.named_scope("bands"):
        started(lin.at[0 : nlat - 1], got.at[L_R]).wait()
    total = lin[0]
    for b in range(1, nlat):
        total = total + lin[b]
    total = total * (1.0 / (NLAT * NLON))
    over = pltpu.roll(total, 128 - 9, 1)
    under = pltpu.roll(total, 128 - 18, 1)
    skill = total / jnp.sqrt(jnp.maximum(over, FLOOR) * jnp.maximum(under, FLOOR))
    measures = jnp.where(lane < 9, jnp.sqrt(jnp.maximum(total, FLOOR)), jnp.where(lane < 18, total, skill))
    hall[j] = jnp.where(lane < SCORES, measures, 0.0)
    for d in range(1, Y * Z):
        to_all(d).start()

    for k in near:
        from_y(k)
    with jax.named_scope("globals"):
        started(hall.at[0 : Y * Z - 1], got.at[H_R]).wait()
    table = hall[:, 0, :]
    owner = lax.broadcasted_iota(jnp.int32, (Y * Z, 128), 0)
    var = lax.broadcasted_iota(jnp.int32, (Y * Z, 128), 1)
    chosen = []
    for l in range(LEADS):
        mine = lax.shift_right_logical((var * LEADS + l) * 7282, 16)
        chosen.append(jnp.where(mine == owner, 1.0, 0.0))
    every = lax.dot_general(
        table,
        jnp.concatenate(chosen, axis=1),
        (((0,), (0,)), ((), ())),
        precision=lax.Precision.HIGHEST,
        preferred_element_type=f32,
    )
    for l in range(LEADS):
        q = var * LEADS + l
        picked = every[0 : Y * Z, 128 * l : 128 * (l + 1)]
        rest = q - lax.shift_right_logical(q * 7282, 16) * PAIRS
        for m, g in enumerate((g0, g1, g2)):
            line = jnp.sum(jnp.where(owner == rest + m * PAIRS, picked, 0.0), axis=0, keepdims=True)
            g[l : l + 1, :] = line[:, 0:VARS]

    with jax.named_scope("gather_o"):
        started(gath.at[0, 0 : Z * SCORES], got.at[OPP_R]).wait()

    with jax.named_scope("sends"):
        for i, ref in (
            (REL, rel),
            (DIR, rel),
            (FWD, rel),
            (TRU, ptru.at[0 : 3 * GV]),
            (ZS, zin),
            (AS, gath.at[0, 0 : (Z - 1) * SCORES]),
            (UPS, gath.at[0, 0 : Z * SCORES]),
            (DOWNS, gath.at[0, 0 : Z * SCORES]),
            (OPPS, gath.at[0, 0 : Z * SCORES]),
            (LS, hall.at[0 : nlat - 1]),
            (HS, hall.at[0 : Y * Z - 1]),
        ):
            started(ref, sent.at[i]).wait()


def writer(gath, s0, s1, s2, o0, o1, o2, g0, g1, g2, sems):
    rows = LEADS * VARS
    copies = [
        pltpu.make_async_copy(gath.at[m, pl.ds(0, rows)], o.reshape(rows, 128), sems.at[m])
        for m, o in enumerate((o0, o1, o2))
    ]
    copies += [
        pltpu.make_async_copy(s, g, sems.at[3 + m]) for m, (s, g) in enumerate(((s0, g0), (s1, g1), (s2, g2)))
    ]
    for c in copies:
        c.start()
    for c in copies:
        c.wait()


def local(prediction_fields, verifying_state, normal_state, evaluated_point_flag, parallels_each_strip):
    f32 = jnp.float32
    hbm, vmem = pl.BlockSpec(memory_space=pltpu.HBM), pl.BlockSpec(memory_space=pltpu.VMEM)
    dma = pltpu.SemaphoreType.DMA
    single = [jax.ShapeDtypeStruct((LEADS, VARS), f32)] * 3
    gathered, *means = pl.pallas_call(
        kernel,
        out_shape=[jax.ShapeDtypeStruct((3, PADDED, 128), f32)] + single,
        in_specs=[hbm] * 5,
        out_specs=[vmem] * 4,
        scratch_shapes=[
            pltpu.VMEM((TILES, 8, LONS, LEADS, 128), f32),
            pltpu.VMEM((TILES, 2, LONS, 8, 128), f32),
            pltpu.VMEM((LONS, 128), jnp.int32),
            pltpu.SMEM((8,), jnp.int32),
            pltpu.VMEM((LONS, 8, 128), jnp.int32),
            pltpu.VMEM((1, 128), f32),
            pltpu.VMEM((4, PADDED, 128), f32),
            pltpu.VMEM((Y * GV, 128), f32),
            *[pltpu.VMEM((Z, 4, PAIRS, 128), f32), pltpu.VMEM((GV, 128), f32)] * 3,
            pltpu.VMEM((GV, 128), f32),
            pltpu.VMEM((Z - 1, ROWS, 128), f32),
            pltpu.VMEM((Z - 1, ROWS, 128), f32),
            pltpu.VMEM((48, 128), f32),
            pltpu.VMEM((8, 1, 128), f32),
            pltpu.VMEM((Y * Z, 1, 128), f32),
            dma((2, TILES)),
            dma((2,)),
            *[dma((Z + 1,))] * 2,
            dma((Z - 1,)),
            dma((Z,)),
            dma((11,)),
            dma((7,)),
        ],
        compiler_params=pltpu.CompilerParams(
            collective_id=0, has_side_effects=True, vmem_limit_bytes=32 * 1024 * 1024
        ),
    )(
        *(
            pltpu.with_memory_space_constraint(x, pltpu.HBM)
            for x in (
                jnp.transpose(prediction_fields, (1, 2, 0, 3)),
                jnp.transpose(verifying_state, (1, 0, 2)),
                jnp.transpose(normal_state, (1, 0, 2)),
                evaluated_point_flag,
                parallels_each_strip,
            )
        )
    )
    *zonal, a, b, c = pl.pallas_call(
        writer,
        out_shape=[jax.ShapeDtypeStruct((VARS, LEADS, 128), f32)] * 3 + single,
        in_specs=[vmem] * 4,
        out_specs=[hbm] * 6,
        scratch_shapes=[dma((6,))],
        compiler_params=pltpu.CompilerParams(vmem_limit_bytes=2 * 1024 * 1024),
    )(gathered, *means)
    return (*(jnp.transpose(o, (1, 0, 2)) for o in zonal), a, b, c)


def solution(mesh):
    placed = (P(None, None, "lon", "lat"), P(None, "lon", "lat"), P(None, "lon", "lat"), P("lon", "lat"), P())
    return jax.shard_map(
        local,
        mesh=mesh,
        in_specs=placed,
        out_specs=(P(None, None, "lat"), P(None, None, "lat"), P(None, None, "lat"), P(), P(), P()),
        check_vma=False,
    )
```

time: 40.3 us -> 36.9 us (0.916); the launches traced: 39.7 us -> 36.8 us
  Pallas kernels: 37.7 us -> 36.1 us
  local copies, waits for them, and re-layouts: 1.39 us -> 0 us
    pallas_call x1, Pallas kernels: 36.9 us -> 35.3 us  [local(): pl.pallas_call(kernel, out_shape=[jax.ShapeDtypeStruct((3, PADDED, 128),...]
    unnamed x4 -> x0, local copies, waits for them, and re-layouts: 1.39 us -> none
where the time goes in v3:
time: 36.9 us; the launch traced here: 36.8 us
  Pallas kernels  36.1 us (98%)
  between operations  0.64 us (2%)
    pallas_call x1, Pallas kernels, local(): pl.pallas_call(kernel, out_shape=[jax.ShapeDtypeStruct((3, PADDED, 128),...  35.3 us
    pallas_call x1, Pallas kernels, local(): pl.pallas_call(writer, out_shape=[jax.ShapeDtypeStruct((VARS, LEADS, 128)...  0.81 us

profile of v3, /device:TPU:2, one launch (start us, length us, event | category | flops | bytes accessed | tf_op | source)
XLA Modules:
  0.0 36.8 jit_solution(4672547989157155891)
XLA Ops:
  0.6 35.3 %shard_map.100 = (f32[3,288,128]{2,1,0:T(8,128)S(1)}, f32[4,69]{1,0:T(4,128)S(1)}, f32[4,69]{1,0:T(4,128)S(1)}, f32[4,69]{1,0:T(4,128)S(1)}) custom-call(f32[69,45,4,128]{3,2,1,0:T(4,128)} %bitcast.6, f32[45,69,128]{2,1,0:T(8,128)} %bitcast.7, f32[45,69,128]{2,1,0:T(8,128)} %bitcast.8, s32[45,128]{1,0:T(8,128)} %flag.1, s32[8]{0:T(128)} %bands.1), custom_call_target="tpu_custom_call" | custom-call | tf_op jit(solution)/shard_map/pallas_call | solution.py:373
  36.0 0.8 %shard_map.101 = (f32[69,4,128]{2,1,0:T(4,128)}, f32[69,4,128]{2,1,0:T(4,128)}, f32[69,4,128]{2,1,0:T(4,128)}, f32[4,69]{1,0:T(4,128)}, f32[4,69]{1,0:T(4,128)}, /*index=5*/f32[4,69]{1,0:T(4,128)}) custom-call(f32[3,288,128]{2,1,0:T(8,128)S(1)} %get-tuple-element.16.gath, f32[4,69]{1,0:T(4,128)S(1)} %get-tuple-element.17.s0, ...), custom_call_target="tpu_custom_call" | custom-call | tf_op jit(solution)/shard_map/pallas_call | solution.py:417

commit v4 on v3

--- a/solution.py
+++ b/solution.py
@@ -24,7 +24,7 @@
 
 def kernel(p, t, n, flag, bands, gath, g0, g1, g2,
            pbuf, tnbuf, fbuf, brow, kbuf, wbuf, part, ptru, rel, rel_t, in_m, in_mt, in_p, in_pt, tsum, zout, zin, sbuf,
-           lin, hall, lsem, fsem, rel_r, fwd_r, a_r, y_r, sent, got):
+           lin, hall, lsem, fsem, rel_r, fwd_r, a_r, y_r, sent, got, known):
     lat, j = lax.axis_index("lat"), lax.axis_index("lon")
     nlat = 8
     y, z = j // Z, lax.rem(j, Z)
@@ -66,10 +66,20 @@
     )
 
     barrier = pltpu.get_barrier_semaphore()
-    for d in range(1, nlat):
-        pl.semaphore_signal(barrier, inc=1, device_id=(lax.rem(lat + d, nlat), j), device_id_type=MESH)
-    for d in range(1, Y * Z):
-        pl.semaphore_signal(barrier, inc=1, device_id=(lat, lax.rem(j + d, Y * Z)), device_id_type=MESH)
+    Z1, Z2, Y1, Y2, L1, L2 = range(6)
+    along_y = [(lat, at(up, z)), (lat, at(down, z))]
+
+    def ring(d):
+        return [(lat, at(y, lax.rem(z + d, Z))), (lat, at(y, lax.rem(z + Z - d, Z)))]
+
+    other_core = (lat + 1 - 2 * lax.rem(lat, 2), j)
+    bands_near = [other_core, (lax.rem(lat + 2, nlat), j), (lax.rem(lat + nlat - 2, nlat), j)]
+
+    def tell(sem, devices):
+        for dev in devices:
+            pl.semaphore_signal(sem, inc=1, device_id=dev, device_id_type=MESH)
+
+    tell(barrier, along_y + ring(1) + bands_near)
 
     def start_loads(phase):
         first, count = phases[phase]
@@ -97,9 +107,6 @@
     lane = lax.broadcasted_iota(jnp.int32, (1, 128), 1)
     for lon in range(LONS):
         kbuf[lon] = jnp.broadcast_to(jnp.where(lane < held, fbuf[lon : lon + 1], 0), (8, 128))
-    angle = (first + lane).astype(f32) * (math.pi / (NLAT - 1))
-    wbuf[...] = jnp.where(lane < held, jnp.sin(angle) * (NLAT / SIN_SUM), 0.0)
-
     prows = pbuf.reshape(TILES * 8 * LONS * LEADS, 128)
 
     def sums(tile):
@@ -179,19 +186,31 @@
     with jax.named_scope("compute_a"):
         compute(0)
     with jax.named_scope("barrier"):
-        pl.semaphore_wait(barrier, Y * Z - 1 + nlat - 1)
+        pl.semaphore_wait(barrier, 7)
     for k in each:
         to_relay(k).start()
+    tell(known.at[Z1], ring(1))
+    tell(known.at[L1], bands_near)
     with jax.named_scope("compute_b"):
         compute(1)
     for k in range(1, Z, 2):
         direct(k).start()
+    with jax.named_scope("known_1"):
+        pl.semaphore_wait(known.at[Z1], 2)
+        tell(known.at[Z2], ring(2))
+        pl.semaphore_wait(known.at[L1], 3)
+        tell(known.at[L2], [other_core])
     with jax.named_scope("compute_c"):
         compute(2)
     for k in (Z, *range(0, Z, 2)):
         direct(k).start()
+    with jax.named_scope("known_2"):
+        pl.semaphore_wait(known.at[Z2], 2)
+        tell(known.at[Y1], along_y)
     with jax.named_scope("compute_d"):
         compute(3)
+    angle = (first + lane).astype(f32) * (math.pi / (NLAT - 1))
+    wbuf[...] = jnp.where(lane < held, jnp.sin(angle) * (NLAT / SIN_SUM), 0.0)
     for k in each:
         with jax.named_scope(f"relay#k={k}"):
             to_relay(k).wait_recv()
@@ -202,6 +221,10 @@
                 part[:, pl.ds(PAIRS * at(g, zto(k)), PAIRS), :] = take(g, k) + rel[k]
             relayed(k).start()
 
+    with jax.named_scope("known_3"):
+        pl.semaphore_wait(known.at[Y1], 2)
+        tell(known.at[Y2], along_y)
+        pl.semaphore_wait(known.at[L2], 1)
     direct(Z).wait_recv()
     relayed(Z).wait_recv()
     started(in_m.at[0:4], got.at[DIR_UP]).wait()
@@ -221,6 +244,7 @@
             along_z(k).start()
     summed(Z - 1, sbuf)
     s = sbuf[0:ROWS]
+    pl.semaphore_wait(known.at[Y2], 2)
     with jax.named_scope("sum_z"):
         started(zin, got.at[Z_R]).wait()
     for k in range(Z - 1):
@@ -398,6 +422,7 @@
             dma((Z,)),
             dma((11,)),
             dma((7,)),
+            pltpu.SemaphoreType.REGULAR((6,)),
         ],
         compiler_params=pltpu.CompilerParams(
             collective_id=0, has_side_effects=True, vmem_limit_bytes=32 * 1024 * 1024

time: 36.9 us -> 35.2 us (0.954)
  Pallas kernels: 36.1 us -> 34.5 us
    pallas_call x1, Pallas kernels: 35.3 us -> 33.7 us  [local(): pl.pallas_call(kernel, out_shape=[jax.ShapeDtypeStruct((3, PADDED, 128),...]
where the time goes in v4:
time: 35.2 us
  Pallas kernels  34.5 us (98%)
  between operations  0.64 us (2%)
    pallas_call x1, Pallas kernels, local(): pl.pallas_call(kernel, out_shape=[jax.ShapeDtypeStruct((3, PADDED, 128),...  33.7 us
    pallas_call x1, Pallas kernels, local(): pl.pallas_call(writer, out_shape=[jax.ShapeDtypeStruct((VARS, LEADS, 128)...  0.81 us

profile of v4, /device:TPU:2, one launch (start us, length us, event | category | flops | bytes accessed | tf_op | source)
XLA Modules:
  0.0 35.2 jit_solution(14670141213697087312)
XLA Ops:
  0.6 33.7 %shard_map.100 = (f32[3,288,128]{2,1,0:T(8,128)S(1)}, f32[4,69]{1,0:T(4,128)S(1)}, f32[4,69]{1,0:T(4,128)S(1)}, f32[4,69]{1,0:T(4,128)S(1)}) custom-call(f32[69,45,4,128]{3,2,1,0:T(4,128)} %bitcast.6, f32[45,69,128]{2,1,0:T(8,128)} %bitcast.7, f32[45,69,128]{2,1,0:T(8,128)} %bitcast.8, s32[45,128]{1,0:T(8,128)} %flag.1, s32[8]{0:T(128)} %bands.1), custom_call_target="tpu_custom_call" | custom-call | tf_op jit(solution)/shard_map/pallas_call | solution.py:397
  34.3 0.8 %shard_map.101 = (f32[69,4,128]{2,1,0:T(4,128)}, f32[69,4,128]{2,1,0:T(4,128)}, f32[69,4,128]{2,1,0:T(4,128)}, f32[4,69]{1,0:T(4,128)}, f32[4,69]{1,0:T(4,128)}, /*index=5*/f32[4,69]{1,0:T(4,128)}) custom-call(f32[3,288,128]{2,1,0:T(8,128)S(1)} %get-tuple-element.16.gath, f32[4,69]{1,0:T(4,128)S(1)} %get-tuple-element.17.s0, ...), custom_call_target="tpu_custom_call" | custom-call | tf_op jit(solution)/shard_map/pallas_call | solution.py:442

commit v5 on v4

--- a/solution.py
+++ b/solution.py
@@ -195,22 +195,17 @@
         compute(1)
     for k in range(1, Z, 2):
         direct(k).start()
-    with jax.named_scope("known_1"):
-        pl.semaphore_wait(known.at[Z1], 2)
-        tell(known.at[Z2], ring(2))
-        pl.semaphore_wait(known.at[L1], 3)
-        tell(known.at[L2], [other_core])
     with jax.named_scope("compute_c"):
         compute(2)
     for k in (Z, *range(0, Z, 2)):
         direct(k).start()
-    with jax.named_scope("known_2"):
-        pl.semaphore_wait(known.at[Z2], 2)
-        tell(known.at[Y1], along_y)
     with jax.named_scope("compute_d"):
         compute(3)
     angle = (first + lane).astype(f32) * (math.pi / (NLAT - 1))
     wbuf[...] = jnp.where(lane < held, jnp.sin(angle) * (NLAT / SIN_SUM), 0.0)
+    with jax.named_scope("known_1"):
+        pl.semaphore_wait(known.at[Z1], 2)
+        tell(known.at[Z2], ring(2))
     for k in each:
         with jax.named_scope(f"relay#k={k}"):
             to_relay(k).wait_recv()
@@ -221,10 +216,9 @@
                 part[:, pl.ds(PAIRS * at(g, zto(k)), PAIRS), :] = take(g, k) + rel[k]
             relayed(k).start()
 
-    with jax.named_scope("known_3"):
-        pl.semaphore_wait(known.at[Y1], 2)
-        tell(known.at[Y2], along_y)
-        pl.semaphore_wait(known.at[L2], 1)
+    with jax.named_scope("known_2"):
+        pl.semaphore_wait(known.at[Z2], 2)
+        tell(known.at[Y1], along_y)
     direct(Z).wait_recv()
     relayed(Z).wait_recv()
     started(in_m.at[0:4], got.at[DIR_UP]).wait()
@@ -244,7 +238,11 @@
             along_z(k).start()
     summed(Z - 1, sbuf)
     s = sbuf[0:ROWS]
-    pl.semaphore_wait(known.at[Y2], 2)
+    with jax.named_scope("known_3"):
+        pl.semaphore_wait(known.at[L1], 3)
+        tell(known.at[L2], [other_core])
+        pl.semaphore_wait(known.at[Y1], 2)
+        tell(known.at[Y2], along_y)
     with jax.named_scope("sum_z"):
         started(zin, got.at[Z_R]).wait()
     for k in range(Z - 1):
@@ -293,6 +291,7 @@
     def to_all(d):
         return remote(hall.at[j], hall.at[j], sent.at[HS], got.at[H_R], (lat, lax.rem(j + d, Y * Z)))
 
+    pl.semaphore_wait(known.at[L2], 1)
     for d in range(1, nlat):
         to_band(d).start()
     def from_z(k):
@@ -325,6 +324,7 @@
     skill = total / jnp.sqrt(jnp.maximum(over, FLOOR) * jnp.maximum(under, FLOOR))
     measures = jnp.where(lane < 9, jnp.sqrt(jnp.maximum(total, FLOOR)), jnp.where(lane < 18, total, skill))
     hall[j] = jnp.where(lane < SCORES, measures, 0.0)
+    pl.semaphore_wait(known.at[Y2], 2)
     for d in range(1, Y * Z):
         to_all(d).start()
 

time: 35.2 us -> 33.9 us (0.963)
  Pallas kernels: 34.5 us -> 33.2 us
    pallas_call x1, Pallas kernels: 33.7 us -> 32.4 us  [local(): pl.pallas_call(kernel, out_shape=[jax.ShapeDtypeStruct((3, PADDED, 128),...]
where the time goes in v5:
time: 33.9 us; the launch traced here: 33.8 us
  Pallas kernels  33.2 us (98%)
  between operations  0.64 us (2%)
    pallas_call x1, Pallas kernels, local(): pl.pallas_call(kernel, out_shape=[jax.ShapeDtypeStruct((3, PADDED, 128),...  32.4 us
    pallas_call x1, Pallas kernels, local(): pl.pallas_call(writer, out_shape=[jax.ShapeDtypeStruct((VARS, LEADS, 128)...  0.81 us

profile of v5, /device:TPU:2, one launch (start us, length us, event | category | flops | bytes accessed | tf_op | source)
XLA Modules:
  0.0 33.8 jit_solution(10196446838351855987)
XLA Ops:
  0.6 32.4 %shard_map.100 = (f32[3,288,128]{2,1,0:T(8,128)S(1)}, f32[4,69]{1,0:T(4,128)S(1)}, f32[4,69]{1,0:T(4,128)S(1)}, f32[4,69]{1,0:T(4,128)S(1)}) custom-call(f32[69,45,4,128]{3,2,1,0:T(4,128)} %bitcast.6, f32[45,69,128]{2,1,0:T(8,128)} %bitcast.7, f32[45,69,128]{2,1,0:T(8,128)} %bitcast.8, s32[45,128]{1,0:T(8,128)} %flag.1, s32[8]{0:T(128)} %bands.1), custom_call_target="tpu_custom_call" | custom-call | tf_op jit(solution)/shard_map/pallas_call | solution.py:397
  33.0 0.8 %shard_map.101 = (f32[69,4,128]{2,1,0:T(4,128)}, f32[69,4,128]{2,1,0:T(4,128)}, f32[69,4,128]{2,1,0:T(4,128)}, f32[4,69]{1,0:T(4,128)}, f32[4,69]{1,0:T(4,128)}, /*index=5*/f32[4,69]{1,0:T(4,128)}) custom-call(f32[3,288,128]{2,1,0:T(8,128)S(1)} %get-tuple-element.16.gath, f32[4,69]{1,0:T(4,128)S(1)} %get-tuple-element.17.s0, ...), custom_call_target="tpu_custom_call" | custom-call | tf_op jit(solution)/shard_map/pallas_call | solution.py:442
